TPU v7x, 32 devices: a whole 2x2x4 slice. The times are simulated.
32 devices in a mesh: replica: 2 (over x), expert: 8 (over z, y), sub: 2 (over core).
Axes of the slice: x: 2, y: 2, z: 4, core: 2. Of those that a mesh axis runs over, the one named last changes fastest.
Arguments:
- tokens: bfloat16 [256, 7168], P(('replica', 'expert', 'sub')), parts along dimension 0, may hold values from -6 to 6
- expert_ids: int32 [256, 2], P(('replica', 'expert', 'sub')), parts along dimension 0, may hold values from 0 to 3, all different within a row; in each aligned block of 8 rows (0 to 7, 8 to 15, ...) at most 6 rows name the same one
- route_levels: int32 [256, 2], P(('replica', 'expert', 'sub')), parts along dimension 0, may hold values from 1 to 255
- gate_proj: bfloat16 [8, 7168, 512], P('expert', None, 'sub'), may hold values from -0.0625 to 0.0625
- up_proj: bfloat16 [8, 7168, 512], P('expert', None, 'sub'), may hold values from -0.0625 to 0.0625
- down_proj: bfloat16 [8, 512, 7168], P('expert', 'sub'), may hold values from -0.1875 to 0.1875
Outputs:
- moe_out: bfloat16 [256, 7168], P(('replica', 'expert', 'sub')), parts along dimension 0
There are 2 independent parts, one for each index of `replica`. A program takes and returns all parts, laid end to end along the dimension named above; an argument that names none is the same for every part. Nothing has to cross between parts.
Inputs may be any that keep to these rules, and one draw needn't show every extreme that they name: `expert_ids`: each row names 2 different experts; among the 8 rows of one device no expert is named more than 6 times, and in some devices' rows one is named exactly 6 times.
All inputs are finite; a program needn't handle non-finite values.
Results may differ from a plain program's by a relative error of at most 0.013.
Values may be sent and summed in bfloat16 or wider, within the bound.
A program may use at most 448 MiB of HBM per device.

v0:
```python
import jax
import jax.numpy as jnp
from jax import lax
from jax.sharding import PartitionSpec as P


def local(tokens, expert_ids, route_levels, gate_proj, up_proj, down_proj):
    rows_here, width = tokens.shape
    picks = expert_ids.shape[1]
    experts = lax.axis_size("expert") * lax.axis_size("sub") // 4
    capacity = rows_here * picks * 3 // (experts * 2)
    pair_count = rows_here * picks
    flat_ids = expert_ids.reshape(pair_count)
    onehot = (flat_ids[:, None] == jnp.arange(experts, dtype=jnp.int32)[None, :]).astype(jnp.int32)
    before = jnp.cumsum(onehot, axis=0, dtype=jnp.int32) - onehot
    slot_of = jnp.sum(before * onehot, axis=1)
    position = flat_ids * capacity + slot_of
    placed = (position[:, None] == jnp.arange(experts * capacity, dtype=jnp.int32)[None, :]).astype(
        jnp.float32
    )
    shares = route_levels.astype(jnp.float32)
    shares = shares / jnp.sum(shares, axis=1, keepdims=True)
    owner_rows = (
        jnp.arange(pair_count, dtype=jnp.int32)[None, :] // picks
        == jnp.arange(rows_here, dtype=jnp.int32)[:, None]
    ).astype(jnp.float32)
    sender = jnp.dot(owner_rows, placed, precision=lax.Precision.HIGHEST)
    weighting = jnp.dot(
        owner_rows * shares.reshape(1, pair_count), placed, precision=lax.Precision.HIGHEST
    )
    outgoing = jnp.dot(sender.T.astype(jnp.bfloat16), tokens, preferred_element_type=jnp.float32)
    outgoing = outgoing.astype(jnp.bfloat16).reshape(experts, 1, capacity, width)
    gate_local = gate_proj[0]
    up_local = up_proj[0]
    down_local = down_proj[0]
    buffer = jnp.broadcast_to(outgoing, (experts, 4, capacity, width)).reshape(
        4 * experts, capacity, width
    )
    arrived = lax.all_to_all(buffer, ("expert", "sub"), split_axis=0, concat_axis=0, tiled=True)
    items = arrived.shape[1]
    leading = arrived.shape[:-1]
    flat_rows = arrived.reshape(-1, width)
    gate_vals = jnp.dot(flat_rows, gate_local, preferred_element_type=jnp.float32)
    up_vals = jnp.dot(flat_rows, up_local, preferred_element_type=jnp.float32)
    hidden = (jax.nn.silu(gate_vals) * up_vals).astype(jnp.bfloat16)
    terms = jnp.dot(hidden, down_local, preferred_element_type=jnp.float32).astype(jnp.bfloat16)
    terms = terms.reshape(leading + (width,)).reshape(-1, 2, items, width)
    groups, _, items, _ = terms.shape
    flat_terms = terms.reshape(2 * groups, items, width)
    returned = lax.all_to_all(
        flat_terms, ("expert", "sub"), split_axis=0, concat_axis=0, tiled=True
    )
    results = jnp.sum(returned.reshape(experts, -1, capacity, width), axis=1, dtype=jnp.float32)
    rounded = lax.optimization_barrier(
        results.reshape(experts * capacity, width).astype(jnp.bfloat16)
    )
    mixed = jnp.dot(
        weighting,
        rounded.astype(jnp.float32),
        precision=lax.Precision.HIGHEST,
        preferred_element_type=jnp.float32,
    )
    return mixed.astype(jnp.bfloat16)


def solution(mesh):
    return jax.shard_map(
        local,
        mesh=mesh,
        in_specs=(
            P(("replica", "expert", "sub"), None),
            P(("replica", "expert", "sub"), None),
            P(("replica", "expert", "sub"), None),
            P("expert", None, "sub"),
            P("expert", None, "sub"),
            P("expert", "sub", None),
        ),
        out_specs=P(("replica", "expert", "sub"), None),
        check_vma=False,
    )
```

profile of v0, /device:TPU:15, one launch (start us, length us, event | category | flops | bytes accessed | tf_op | source)
XLA Modules:
  0.0 108.4 jit_solution(5056079490853977356)
XLA Ops:
  0.0 0.0 copy-start
  0.0 0.8 copy.10
  0.8 0.1 reshape.65
  0.9 0.1 fusion.21
  1.0 0.2 select_reduce_fusion
  1.2 0.2 convolution_convert_fusion.3
  1.4 0.0 copy-done
  1.4 0.2 convolution_convert_fusion.1
  1.7 0.1 broadcast_in_dim.4
  1.8 0.2 broadcast_in_dim.5
  2.0 48.0 %all_to_all.10 = bf16[16,6,7168]{2,1,0:T(8,128)(2,1)S(1)} all-to-all(bf16[16,6,7168]{2,1,0:T(8,128)(2,1)S(1)} %bitcast.24), channel_id=1, replica_groups=mesh['replica'=2,'expert'=8,'sub'=2] {'expert','sub'}, dimensions={0} | all-to-all | bytes 2752512 | tf_op jit(solution)/shard_map/all_to_all | solution.py:39
  50.0 0.5 reshape.67
  50.5 2.8 %fusion.3 = f32[96,256]{1,0:T(8,128)S(1)} fusion(bf16[96,7168]{1,0:T(8,128)(2,1)S(1)} %reshape.67, bf16[1,7168,256]{2,1,0:T(8,128)(2,1)} %param.9), kind=kOutput, calls=%fused_computation.6 | convolution fusion | flops 352321536 | bytes 5144576 | tf_op jit(solution)/shard_map/dot_general | solution.py:43
  53.2 5.3 %convolution_convert_fusion = bf16[96,7168]{1,0:T(8,128)(2,1)S(1)} fusion(bf16[1,256,7168]{2,1,0:T(8,128)(2,1)} %param.11, bf16[96,7168]{1,0:T(8,128)(2,1)S(1)} %reshape.67, bf16[1,7168,256]{2,1,0:T(8,128)(2,1)} %param.10, f32[96,256]{1,0:T(8,128)S(1)} %fusion.3), kind=kOutput, calls=%fused_computation | convolution fusion | flops 705478656 | bytes 10190848 | tf_op jit(solution)/shard_map/dot_general | solution.py:46
  58.5 1.5 %reshape_reshape_reshape.3 = bf16[16,6,7168]{2,1,0:T(8,128)(2,1)} reshape(bf16[96,7168]{1,0:T(8,128)(2,1)S(1)} %convolution_convert_fusion) | data formatting | bytes 2752512 | tf_op jit(solution)/shard_map/reshape;reshape;reshape | solution.py:49
  60.1 0.0 copy-start.1
  60.1 5.1 %all-to-all-start.1 = ((bf16[16,6,7168]{2,1,0:T(8,128)(2,1)}), bf16[16,6,7168]{2,1,0:T(8,128)(2,1)S(1)}, u32[]{:S(2)}, u32[]{:S(2)}) async-start(bf16[16,6,7168]{2,1,0:T(8,128)(2,1)} %reshape_reshape_reshape.3), calls=%async_computation.1 | async-start | bytes 3670016 | tf_op jit(solution)/shard_map/all_to_all | solution.py:50
  65.2 0.0 copy-done.1
  65.2 0.1 copy.9
  65.3 0.1 mul.27
  65.4 0.2 fusion.20
  65.6 41.4 %all-to-all-done.1 = bf16[16,6,7168]{2,1,0:T(8,128)(2,1)S(1)} async-done(((bf16[16,6,7168]{2,1,0:T(8,128)(2,1)}), bf16[16,6,7168]{2,1,0:T(8,128)(2,1)S(1)}, u32[]{:S(2)}, u32[]{:S(2)}) %all-to-all-start.1) | async-done | bytes 1376288 | tf_op jit(solution)/shard_map/all_to_all | solution.py:50
  107.0 0.4 bitcast_reduce_fusion
  107.3 0.1 convert_element_type.45
  107.5 0.9 convolution_convert_fusion.2
  (4 shorter events, 0.1 us)
Async XLA Ops:
  0.0 1.4 %copy-start = (bf16[8,7168]{1,0:T(8,128)(2,1)S(1)}, bf16[8,7168]{1,0:T(8,128)(2,1)}, u32[]{:S(2)}) copy-start(bf16[8,7168]{1,0:T(8,128)(2,1)} %param.6) | copy-start | bytes 344068
  60.1 5.1 %copy-start.1 = (s32[8,2]{0,1:T(2,128)S(1)}, s32[8,2]{0,1:T(2,128)}, u32[]{:S(2)}) copy-start(s32[8,2]{0,1:T(2,128)} %param.8) | copy-start | bytes 196
  60.1 46.9 %all-to-all-start.1 = ((bf16[16,6,7168]{2,1,0:T(8,128)(2,1)}), bf16[16,6,7168]{2,1,0:T(8,128)(2,1)S(1)}, u32[]{:S(2)}, u32[]{:S(2)}) async-start(bf16[16,6,7168]{2,1,0:T(8,128)(2,1)} %reshape_reshape_reshape.3), calls=%async_computation.1 | async-start | bytes 3670016 | tf_op jit(solution)/shard_map/all_to_all | solution.py:50
where the time goes:
time: 109 us; the launch traced here: 108 us
  blocking collectives  48 us (44%)
  waiting for transfers between devices  41.4 us (38%)
  matrix products  9.64 us (9%)
  starting transfers between devices  5.12 us (5%)
  local copies, waits for them, and re-layouts  3.52 us (3%)
    all_to_all x1, blocking collectives, local(): lax.all_to_all(buffer, ('expert', 'sub'), split_axis=0, concat_axis=0, ti...  48 us
    all_to_all x1, waiting for transfers between devices, local(): lax.all_to_all(flat_terms, ('expert', 'sub'), split_axis=0, concat_axis=0...  41.4 us
    dot_general x1, matrix products, local(): jnp.dot(hidden, down_local, preferred_element_type=jnp.float32)  5.28 us
    all_to_all x1, starting transfers between devices, local(): lax.all_to_all(flat_terms, ('expert', 'sub'), split_axis=0, concat_axis=0...  5.12 us
    dot_general x1, matrix products, local(): jnp.dot(flat_rows, gate_local, preferred_element_type=jnp.float32)  2.75 us
  transfers between devices with their start and end apart: 1, of which 1 were waited for; matrix products, arithmetic and copies ran while one was open for 0% of the time, Pallas kernels for 0%

commit v1 on v0

--- a/solution.py
+++ b/solution.py
@@ -1,6 +1,9 @@
+import functools
 import jax
 import jax.numpy as jnp
 from jax import lax
+from jax.experimental import pallas as pl
+from jax.experimental.pallas import tpu as pltpu
 from jax.sharding import PartitionSpec as P
 
 
@@ -63,9 +66,218 @@
     return mixed.astype(jnp.bfloat16)
 
 
+MESH = pl.DeviceIdType.MESH
+VMEM_BUDGET = 60 * 1024 * 1024
+
+
+def column_cuts(width, pieces):
+    lanes = width // 128
+    edges = [128 * (lanes * i // pieces) for i in range(pieces + 1)]
+    return [(a, b - a) for a, b in zip(edges[:-1], edges[1:]) if b > a]
+
+
+def fused(groups, p_width, cuts, ids_ref, levels_ref, tok_in, gate_hbm, up_hbm, down_hbm, out_ref,
+          tok, gate_v, up_v, down_v, hid, keep, dsend, drecv, ysend, yrecv, zsend, zrecv,
+          send_sem, recv_sem, local_sem):
+    rows, width = tok_in.shape
+    spot = lax.axis_index("expert")
+    s = lax.axis_index("sub")
+    z, h = spot // 2, spot % 2
+    n = groups
+
+    loads = [pltpu.make_async_copy(src, dst, local_sem.at[i]) for i, (src, dst) in enumerate(
+        ((gate_hbm.at[0], gate_v), (up_hbm.at[0], up_v), (down_hbm.at[0], down_v)))]
+    for load in loads:
+        load.start()
+    tok[spot, s] = tok_in[...]
+
+    def ring(step):
+        return lax.rem(z + step + n, n)
+
+    def at(group, half, core):
+        return {"expert": group * 2 + half, "sub": core}
+
+    sub_peer, half_peer = at(z, h, 1 - s), at(z, 1 - h, s)
+    barrier = pltpu.get_barrier_semaphore()
+    peers = [sub_peer, half_peer] + [at(ring(d), h, s) for d in range(1, n)]
+    for peer in peers:
+        pl.semaphore_signal(barrier, inc=1, device_id=peer, device_id_type=MESH)
+    pl.semaphore_wait(barrier, len(peers))
+
+    count = [0]
+    started = []
+
+    def send(src, dst, peer):
+        i = count[0]
+        count[0] += 1
+        copy = pltpu.make_async_remote_copy(src_ref=src, dst_ref=dst, send_sem=send_sem.at[i],
+                                            recv_sem=recv_sem.at[i], device_id=peer, device_id_type=MESH)
+        copy.start()
+        started.append(copy)
+        return copy
+
+    def block(group, half, cols):
+        return tok.at[group * 2 + half, s, :, pl.ds(cols[0], cols[1])]
+
+    def move(group, half, cols, peer):
+        return send(block(group, half, cols), block(group, half, cols), peer)
+
+    def own(cols, peer):
+        return send(tok_in.at[:, pl.ds(cols[0], cols[1])], block(z, h, cols), peer)
+
+    P, Q = (0, p_width), (p_width, width - p_width)
+    last = []
+
+    def across(group, half, cols):
+        last.append(move(group, half, cols, sub_peer))
+
+    def halves(cols):
+        first = cols[1] // 256 * 128
+        return (cols[0], first), (cols[0] + first, cols[1] - first)
+
+    up_peer, down_peer = at(ring(1), h, s), at(ring(-1), h, s)
+
+    def hop(half, cols, first):
+        def starter(d):
+            a, b = (cols, cols) if 2 * d < n else halves(cols)
+            if d == 1 and first:
+                return [own(a, up_peer), own(b, down_peer)]
+            return [move(ring(1 - d), half, a, up_peer), move(ring(d - 1), half, b, down_peer)]
+        return starter
+
+    y_p = own(P, half_peer)
+    hop_p, hop_q, hop_o = hop(h, P, True), hop(h, Q, True), hop(1 - h, P, False)
+    step_p = hop_p(1)
+    step_q = hop_q(1)
+    y_q = [own(Q, half_peer)]
+    last.append(send(tok_in, tok.at[spot, s], sub_peer))
+    y_p.wait_recv()
+    step_o = hop_o(1)
+    across(z, 1 - h, P)
+    for d in range(1, n // 2 + 1):
+        for name in ("p", "q", "o"):
+            steps = {"p": step_p, "q": step_q, "o": step_o}[name]
+            for copy in steps:
+                copy.wait_recv()
+            cols = Q if name == "q" else P
+            half = 1 - h if name == "o" else h
+            if 2 * d < n:
+                more = {"p": hop_p, "q": hop_q, "o": hop_o}[name](d + 1)
+                if name == "p":
+                    step_p = more
+                elif name == "q":
+                    step_q = more
+                else:
+                    step_o = more
+                arrived = [ring(-d), ring(d)]
+            else:
+                arrived = [ring(d)]
+            for group in arrived:
+                if name == "q":
+                    y_q.append(move(group, half, cols, half_peer))
+                across(group, half, cols)
+    order = [z]
+    for d in range(1, n // 2 + 1):
+        order += [ring(-d), ring(d)] if 2 * d < n else [ring(d)]
+    for copy, group in zip(y_q, order):
+        copy.wait_recv()
+        across(group, 1 - h, Q)
+    for copy in last:
+        copy.wait_recv()
+    for load in loads:
+        load.wait()
+
+    total = 4 * n * rows
+    gate = jnp.zeros((total, gate_v.shape[1]), jnp.float32)
+    up = jnp.zeros((total, up_v.shape[1]), jnp.float32)
+    for start, size in cuts:
+        lhs = tok[:, :, :, start:start + size].reshape(total, size)
+        gate += jnp.dot(lhs, gate_v[start:start + size, :], preferred_element_type=jnp.float32)
+        up += jnp.dot(lhs, up_v[start:start + size, :], preferred_element_type=jnp.float32)
+    hid[...] = (jax.nn.silu(gate) * up).reshape(hid.shape)
+    units = hid.shape[-1]
+    ordered = jnp.concatenate([hid[:, half, core].reshape(n * rows, units)
+                               for core in (1 - s, s) for half in (1 - h, h)], axis=0).astype(jnp.bfloat16)
+
+    part, span = n * rows, max(size for _, size in cuts)
+    d_copies, y_copies, z_copies = [], [], []
+    for c, (start, size) in enumerate(cuts):
+        terms = jnp.dot(ordered, down_v[:, start:start + size], preferred_element_type=jnp.float32)
+        dsend[c] = terms[:2 * part].astype(jnp.bfloat16)
+        keep[c] = terms[2 * part:]
+        d_copies.append(send(dsend.at[c], drecv.at[c], sub_peer))
+    for c in range(len(cuts)):
+        d_copies[c].wait_recv()
+        ysend[c] = (keep[c, :part] + drecv[c, :part].astype(jnp.float32)).astype(jnp.bfloat16)
+        y_copies.append(send(ysend.at[c], yrecv.at[c], half_peer))
+    for c in range(len(cuts)):
+        y_copies[c].wait_recv()
+        sums = (keep[c, part:] + drecv[c, part:].astype(jnp.float32)) + yrecv[c].astype(jnp.float32)
+        zsend[c] = sums.reshape(n, rows, span).astype(jnp.bfloat16)
+        z_copies.append([send(zsend.at[c, ring(d)], zrecv.at[c, d], at(ring(d), h, s)) for d in range(1, n)])
+    levels = levels_ref[...].astype(jnp.float32)
+    shares = levels / jnp.sum(levels, axis=1, keepdims=True)
+    ids = ids_ref[...]
+    weights = [jnp.sum(jnp.where(ids == ring(-d), shares, 0.0), axis=1, keepdims=True) for d in range(n)]
+    for c, (start, size) in enumerate(cuts):
+        mixed = weights[0] * zsend[c, z].astype(jnp.float32)
+        for d in range(1, n):
+            z_copies[c][d - 1].wait_recv()
+            mixed += weights[d] * zrecv[c, d].astype(jnp.float32)
+        out_ref[:, start:start + size] = mixed.astype(out_ref.dtype)
+    for copy in started:
+        copy.wait_send()
+
+
+def fused_local(tokens, expert_ids, route_levels, gate_proj, up_proj, down_proj):
+    rows, width = tokens.shape
+    n = lax.axis_size("expert") // 2
+    units = gate_proj.shape[2]
+    pieces = 7
+    cuts = column_cuts(width, pieces)
+    nc, span, part = len(cuts), cuts[0][1], n * rows
+    bf, f32 = jnp.bfloat16, jnp.float32
+    vmem = pl.BlockSpec(memory_space=pltpu.VMEM)
+    hbm = pl.BlockSpec(memory_space=pl.ANY)
+    messages = 160
+    return pl.pallas_call(
+        functools.partial(fused, n, width * 4 // 7 // 128 * 128, cuts),
+        out_shape=jax.ShapeDtypeStruct((rows, width), bf),
+        in_specs=[vmem, vmem, vmem, hbm, hbm, hbm],
+        out_specs=vmem,
+        scratch_shapes=[
+            pltpu.VMEM((2 * n, 2, rows, width), bf),
+            pltpu.VMEM((width, units), bf),
+            pltpu.VMEM((width, units), bf),
+            pltpu.VMEM((units, width), bf),
+            pltpu.VMEM((n, 2, 2, rows, units), f32),
+            pltpu.VMEM((nc, 2 * part, span), f32),
+            pltpu.VMEM((nc, 2 * part, span), bf),
+            pltpu.VMEM((nc, 2 * part, span), bf),
+            pltpu.VMEM((nc, part, span), bf),
+            pltpu.VMEM((nc, part, span), bf),
+            pltpu.VMEM((nc, n, rows, span), bf),
+            pltpu.VMEM((nc, n, rows, span), bf),
+            pltpu.SemaphoreType.DMA((messages,)),
+            pltpu.SemaphoreType.DMA((messages,)),
+            pltpu.SemaphoreType.DMA((3,)),
+        ],
+        compiler_params=pltpu.CompilerParams(collective_id=0, has_side_effects=True, vmem_limit_bytes=VMEM_BUDGET),
+    )(expert_ids, route_levels, tokens, gate_proj, up_proj, down_proj)
+
+
+def whole(tokens, expert_ids, route_levels, gate_proj, up_proj, down_proj):
+    rows, width = tokens.shape
+    groups = lax.axis_size("expert") // 2
+    held = groups * rows * width * 64 + 6 * width * gate_proj.shape[2]
+    if groups % 2 == 0 and lax.axis_size("sub") == 2 and width % (7 * 128) == 0 and held < VMEM_BUDGET:
+        return fused_local(tokens, expert_ids, route_levels, gate_proj, up_proj, down_proj)
+    return local(tokens, expert_ids, route_levels, gate_proj, up_proj, down_proj)
+
+
 def solution(mesh):
     return jax.shard_map(
-        local,
+        whole,
         mesh=mesh,
         in_specs=(
             P(("replica", "expert", "sub"), None),

time: 109 us -> 49.7 us (0.46)
  the two profiles are of different devices: /device:TPU:15 before, /device:TPU:0 now
where the time goes in v1:
time: 49.7 us; the launch traced here: 49.5 us
  Pallas kernels  45.3 us (91%)
  local copies, waits for them, and re-layouts  4.24 us (9%)
    pallas_call x1, Pallas kernels, fused_local(): pl.pallas_call(functools.partial(fused, n, width * 4 // 7 // 128 * 128, c...  45.3 us
    unnamed x3, local copies, waits for them, and re-layouts  4.24 us

profile of v1, /device:TPU:0, one launch (start us, length us, event | category | flops | bytes accessed | tf_op | source)
XLA Modules:
  0.0 49.5 jit_solution(17690910111539617708)
XLA Ops:
  0.0 1.3 %copy.7.ids_ref = s32[8,2]{1,0:T(8,128)} copy(s32[8,2]{0,1:T(2,128)} %param.7) | data formatting | bytes 128 | tf_op args[1]
  1.3 1.3 %copy.8.levels_ref = s32[8,2]{1,0:T(8,128)} copy(s32[8,2]{0,1:T(2,128)} %param.8) | data formatting | bytes 128 | tf_op args[2]
  2.7 45.3 %shard_map.64 = bf16[8,7168]{1,0:T(8,128)(2,1)} custom-call(s32[8,2]{1,0:T(8,128)} %copy.7.ids_ref, s32[8,2]{1,0:T(8,128)} %copy.8.levels_ref, bf16[8,7168]{1,0:T(8,128)(2,1)} %tok_in.1, bf16[1,7168,256]{2,1,0:T(8,128)(2,1)} %gate_hbm.1, bf16[1,7168,256]{2,1,0:T(8,128)(2,1)} %up_hbm.1, bf16[1,256,7168]{2,1,0:T(8,128)(2,1)} %down_hbm.1), custom_call_target="tpu_custom_call" | custom-call | tf_op jit(solution)/shard_map/pallas_call | solution.py:243
  48.0 1.6 %copy.10 = bf16[8,7168]{1,0:T(8,128)(2,1)} copy(bf16[8,7168]{1,0:T(8,128)(2,1)} %shard_map.64) | data formatting | bytes 229376

commit v2 on v1

--- a/solution.py
+++ b/solution.py
@@ -76,114 +76,136 @@
     return [(a, b - a) for a, b in zip(edges[:-1], edges[1:]) if b > a]
 
 
-def fused(groups, p_width, cuts, ids_ref, levels_ref, tok_in, gate_hbm, up_hbm, down_hbm, out_ref,
-          tok, gate_v, up_v, down_v, hid, keep, dsend, drecv, ysend, yrecv, zsend, zrecv,
+def column_cuts_from(start, width, pieces):
+    return [(start + a, size) for a, size in column_cuts(width - start, pieces)]
+
+
+def fused(groups, first_cols, rest_cols, cuts, ids_hbm, levels_hbm, tok_hbm, gate_hbm, up_hbm, down_hbm, out_ref,
+          ids_ref, levels_ref, tok, gate_v, up_v, down_v, hid, keep, dsend, drecv, ysend, yrecv, zsend, zrecv,
           send_sem, recv_sem, local_sem):
-    rows, width = tok_in.shape
+    rows, width = tok_hbm.shape
     spot = lax.axis_index("expert")
     s = lax.axis_index("sub")
     z, h = spot // 2, spot % 2
     n = groups
 
-    loads = [pltpu.make_async_copy(src, dst, local_sem.at[i]) for i, (src, dst) in enumerate(
-        ((gate_hbm.at[0], gate_v), (up_hbm.at[0], up_v), (down_hbm.at[0], down_v)))]
+    first_load = pltpu.make_async_copy(tok_hbm, tok.at[spot, s], local_sem.at[0])
+    first_load.start()
+    loads = [pltpu.make_async_copy(src, dst, local_sem.at[i + 1]) for i, (src, dst) in enumerate(
+        ((ids_hbm, ids_ref), (levels_hbm, levels_ref),
+         (gate_hbm.at[0], gate_v), (up_hbm.at[0], up_v), (down_hbm.at[0], down_v)))]
+
+    def ring(step):
+        return lax.rem(z + step + n, n)
+
+    def at(group, half, core):
+        return {"expert": group * 2 + half, "sub": core}
+
+    sub_peer, half_peer = at(z, h, 1 - s), at(z, 1 - h, s)
+    above, below = z + 1 < n, z > 0
+    barrier = pltpu.get_barrier_semaphore()
+
+    def greet(peer):
+        pl.semaphore_signal(barrier, inc=1, device_id=peer, device_id_type=MESH)
+
+    pl.when(above)(lambda: greet(at(z + 1, h, s)))
+    pl.when(below)(lambda: greet(at(z - 1, h, s)))
+    greet(half_peer)
+    greet(sub_peer)
     for load in loads:
         load.start()
-    tok[spot, s] = tok_in[...]
-
-    def ring(step):
-        return lax.rem(z + step + n, n)
-
-    def at(group, half, core):
-        return {"expert": group * 2 + half, "sub": core}
-
-    sub_peer, half_peer = at(z, h, 1 - s), at(z, 1 - h, s)
-    barrier = pltpu.get_barrier_semaphore()
-    peers = [sub_peer, half_peer] + [at(ring(d), h, s) for d in range(1, n)]
-    for peer in peers:
-        pl.semaphore_signal(barrier, inc=1, device_id=peer, device_id_type=MESH)
-    pl.semaphore_wait(barrier, len(peers))
+    first_load.wait()
+    pl.semaphore_wait(barrier, 2 + above.astype(jnp.int32) + below.astype(jnp.int32))
 
     count = [0]
-    started = []
+    endings = []
+
+    def copy_of(i, src, dst, peer):
+        return pltpu.make_async_remote_copy(src_ref=src, dst_ref=dst, send_sem=send_sem.at[i],
+                                            recv_sem=recv_sem.at[i], device_id=peer, device_id_type=MESH)
 
     def send(src, dst, peer):
         i = count[0]
         count[0] += 1
-        copy = pltpu.make_async_remote_copy(src_ref=src, dst_ref=dst, send_sem=send_sem.at[i],
-                                            recv_sem=recv_sem.at[i], device_id=peer, device_id_type=MESH)
+        copy = copy_of(i, src, dst, peer)
         copy.start()
-        started.append(copy)
+        endings.append(copy.wait_send)
         return copy
 
     def block(group, half, cols):
         return tok.at[group * 2 + half, s, :, pl.ds(cols[0], cols[1])]
 
-    def move(group, half, cols, peer):
-        return send(block(group, half, cols), block(group, half, cols), peer)
-
-    def own(cols, peer):
-        return send(tok_in.at[:, pl.ds(cols[0], cols[1])], block(z, h, cols), peer)
-
-    P, Q = (0, p_width), (p_width, width - p_width)
-    last = []
-
-    def across(group, half, cols):
-        last.append(move(group, half, cols, sub_peer))
-
-    def halves(cols):
-        first = cols[1] // 256 * 128
-        return (cols[0], first), (cols[0] + first, cols[1] - first)
-
-    up_peer, down_peer = at(ring(1), h, s), at(ring(-1), h, s)
-
-    def hop(half, cols, first):
-        def starter(d):
-            a, b = (cols, cols) if 2 * d < n else halves(cols)
-            if d == 1 and first:
-                return [own(a, up_peer), own(b, down_peer)]
-            return [move(ring(1 - d), half, a, up_peer), move(ring(d - 1), half, b, down_peer)]
-        return starter
-
-    y_p = own(P, half_peer)
-    hop_p, hop_q, hop_o = hop(h, P, True), hop(h, Q, True), hop(1 - h, P, False)
-    step_p = hop_p(1)
-    step_q = hop_q(1)
-    y_q = [own(Q, half_peer)]
-    last.append(send(tok_in, tok.at[spot, s], sub_peer))
-    y_p.wait_recv()
-    step_o = hop_o(1)
-    across(z, 1 - h, P)
-    for d in range(1, n // 2 + 1):
-        for name in ("p", "q", "o"):
-            steps = {"p": step_p, "q": step_q, "o": step_o}[name]
-            for copy in steps:
-                copy.wait_recv()
-            cols = Q if name == "q" else P
-            half = 1 - h if name == "o" else h
-            if 2 * d < n:
-                more = {"p": hop_p, "q": hop_q, "o": hop_o}[name](d + 1)
-                if name == "p":
-                    step_p = more
-                elif name == "q":
-                    step_q = more
-                else:
-                    step_o = more
-                arrived = [ring(-d), ring(d)]
+    def when_send(group, half, cols, peer, cond):
+        i = count[0]
+        count[0] += 1
+        part_of = block(group, half, cols)
+        copy = copy_of(i, part_of, part_of, peer)
+
+        def do(action):
+            if cond is None:
+                action()
             else:
-                arrived = [ring(d)]
-            for group in arrived:
-                if name == "q":
-                    y_q.append(move(group, half, cols, half_peer))
-                across(group, half, cols)
-    order = [z]
-    for d in range(1, n // 2 + 1):
-        order += [ring(-d), ring(d)] if 2 * d < n else [ring(d)]
-    for copy, group in zip(y_q, order):
-        copy.wait_recv()
-        across(group, 1 - h, Q)
-    for copy in last:
-        copy.wait_recv()
+                pl.when(cond)(action)
+        do(copy.start)
+        endings.append(lambda: do(copy.wait_send))
+        return i
+
+    def when_arrived(i, group, half, cols, cond):
+        part_of = block(group, half, cols)
+        copy = copy_of(i, part_of, part_of, sub_peer)
+        if cond is None:
+            copy.wait_recv()
+        else:
+            pl.when(cond)(copy.wait_recv)
+
+    def climb(d, half, cols):
+        return (when_send(z - d + 1, half, cols, at(z + 1, h, s), above & (z - d + 1 >= 0)),
+                when_send(z + d - 1, half, cols, at(z - 1, h, s), below & (z + d - 1 < n)))
+
+    crossing, turning = [], []
+
+    def across(group, half, cols, cond=None):
+        crossing.append((when_send(group, half, cols, sub_peer, cond), group, half, cols, cond))
+
+    def turn(group, cols, cond=None):
+        turning.append((when_send(group, h, cols, half_peer, cond), group, 1 - h, cols, cond))
+
+    def turned(amount):
+        for _ in range(amount):
+            item = turning.pop(0)
+            when_arrived(*item)
+            across(*item[1:])
+
+    first_turn = [when_send(z, h, cols, half_peer, None) for cols in first_cols]
+    lines = [(h, cols) for cols in first_cols + rest_cols]
+    steps = [climb(1, half, cols) for half, cols in lines]
+    for cols in rest_cols:
+        turn(z, cols)
+    across(z, h, (0, width))
+    for i, cols in zip(first_turn, first_cols):
+        when_arrived(i, z, 1 - h, cols, None)
+        lines.append((1 - h, cols))
+        steps.append(climb(1, 1 - h, cols))
+        across(z, 1 - h, cols)
+    for d in range(1, n):
+        later = []
+        waiting = len(turning)
+        for (half, cols), (rising, falling) in zip(lines, steps):
+            low, high = z - d >= 0, z + d < n
+            when_arrived(rising, z - d, half, cols, low)
+            when_arrived(falling, z + d, half, cols, high)
+            if d + 1 < n:
+                later.append(climb(d + 1, half, cols))
+            if cols in rest_cols:
+                turn(z - d, cols, low)
+                turn(z + d, cols, high)
+            across(z - d, half, cols, low)
+            across(z + d, half, cols, high)
+        steps = later
+        turned(waiting)
+    turned(len(turning))
+    for item in crossing:
+        when_arrived(*item)
     for load in loads:
         load.wait()
 
@@ -216,17 +238,21 @@
         zsend[c] = sums.reshape(n, rows, span).astype(jnp.bfloat16)
         z_copies.append([send(zsend.at[c, ring(d)], zrecv.at[c, d], at(ring(d), h, s)) for d in range(1, n)])
     levels = levels_ref[...].astype(jnp.float32)
-    shares = levels / jnp.sum(levels, axis=1, keepdims=True)
+    shares = levels / jnp.sum(levels, axis=0, keepdims=True)
     ids = ids_ref[...]
-    weights = [jnp.sum(jnp.where(ids == ring(-d), shares, 0.0), axis=1, keepdims=True) for d in range(n)]
+    eye = (lax.broadcasted_iota(jnp.int32, (rows, rows), 0) == lax.broadcasted_iota(jnp.int32, (rows, rows), 1))
+    weights = []
+    for d in range(n):
+        flat = jnp.sum(jnp.where(ids == ring(-d), shares, 0.0), axis=0, keepdims=True)
+        weights.append(jnp.sum(jnp.where(eye, flat, 0.0), axis=1, keepdims=True))
     for c, (start, size) in enumerate(cuts):
         mixed = weights[0] * zsend[c, z].astype(jnp.float32)
         for d in range(1, n):
             z_copies[c][d - 1].wait_recv()
             mixed += weights[d] * zrecv[c, d].astype(jnp.float32)
         out_ref[:, start:start + size] = mixed.astype(out_ref.dtype)
-    for copy in started:
-        copy.wait_send()
+    for ending in endings:
+        ending()
 
 
 def fused_local(tokens, expert_ids, route_levels, gate_proj, up_proj, down_proj):
@@ -239,13 +265,15 @@
     bf, f32 = jnp.bfloat16, jnp.float32
     vmem = pl.BlockSpec(memory_space=pltpu.VMEM)
     hbm = pl.BlockSpec(memory_space=pl.ANY)
-    messages = 160
+    messages = 240
     return pl.pallas_call(
-        functools.partial(fused, n, width * 4 // 7 // 128 * 128, cuts),
+        functools.partial(fused, n, [cuts[0]], column_cuts_from(cuts[0][1], width, 3), cuts),
         out_shape=jax.ShapeDtypeStruct((rows, width), bf),
-        in_specs=[vmem, vmem, vmem, hbm, hbm, hbm],
+        in_specs=[hbm] * 6,
         out_specs=vmem,
         scratch_shapes=[
+            pltpu.VMEM(expert_ids.shape[::-1], jnp.int32),
+            pltpu.VMEM(expert_ids.shape[::-1], jnp.int32),
             pltpu.VMEM((2 * n, 2, rows, width), bf),
             pltpu.VMEM((width, units), bf),
             pltpu.VMEM((width, units), bf),
@@ -260,10 +288,10 @@
             pltpu.VMEM((nc, n, rows, span), bf),
             pltpu.SemaphoreType.DMA((messages,)),
             pltpu.SemaphoreType.DMA((messages,)),
-            pltpu.SemaphoreType.DMA((3,)),
+            pltpu.SemaphoreType.DMA((6,)),
         ],
         compiler_params=pltpu.CompilerParams(collective_id=0, has_side_effects=True, vmem_limit_bytes=VMEM_BUDGET),
-    )(expert_ids, route_levels, tokens, gate_proj, up_proj, down_proj)
+    )(expert_ids.T, route_levels.T, tokens, gate_proj, up_proj, down_proj)
 
 
 def whole(tokens, expert_ids, route_levels, gate_proj, up_proj, down_proj):

time: 49.7 us -> 43.4 us (0.87)
  Pallas kernels: 45.3 us -> 41.7 us
  local copies, waits for them, and re-layouts: 4.24 us -> 1.55 us
    pallas_call x1, Pallas kernels: 45.3 us -> 41.7 us  [fused_local(): pl.pallas_call(functools.partial(fused, n, [cuts[0]], column_cuts_from(cu...]
    unnamed x3 -> x1, local copies, waits for them, and re-layouts: 4.24 us -> 1.55 us
where the time goes in v2:
time: 43.4 us; the launch traced here: 43.3 us
  Pallas kernels  41.7 us (96%)
  local copies, waits for them, and re-layouts  1.55 us (4%)
    pallas_call x1, Pallas kernels, fused_local(): pl.pallas_call(functools.partial(fused, n, [cuts[0]], column_cuts_from(cu...  41.7 us
    unnamed x1, local copies, waits for them, and re-layouts  1.55 us

profile of v2, /device:TPU:0, one launch (start us, length us, event | category | flops | bytes accessed | tf_op | source)
XLA Modules:
  0.0 43.3 jit_solution(15520622630248355170)
XLA Ops:
  0.0 41.7 %shard_map.64 = bf16[8,7168]{1,0:T(8,128)(2,1)} custom-call(s32[2,8]{1,0:T(2,128)} %bitcast.2, s32[2,8]{1,0:T(2,128)} %bitcast.3, bf16[8,7168]{1,0:T(8,128)(2,1)} %tok_hbm.1, bf16[1,7168,256]{2,1,0:T(8,128)(2,1)} %gate_hbm.1, bf16[1,7168,256]{2,1,0:T(8,128)(2,1)} %up_hbm.1, bf16[1,256,7168]{2,1,0:T(8,128)(2,1)} %down_hbm.1), custom_call_target="tpu_custom_call" | custom-call | tf_op jit(solution)/shard_map/pallas_call | solution.py:269
  41.8 1.6 %copy.8 = bf16[8,7168]{1,0:T(8,128)(2,1)} copy(bf16[8,7168]{1,0:T(8,128)(2,1)} %shard_map.64) | data formatting | bytes 229376

commit v3 on v2

--- a/solution.py
+++ b/solution.py
@@ -80,7 +80,15 @@
     return [(start + a, size) for a, size in column_cuts(width - start, pieces)]
 
 
-def fused(groups, first_cols, rest_cols, cuts, ids_hbm, levels_hbm, tok_hbm, gate_hbm, up_hbm, down_hbm, out_ref,
+def shrinking_cuts(width):
+    shares, lanes, edges = (3, 6, 6, 6, 4, 3), width // 128, [0]
+    for share in shares:
+        edges.append(edges[-1] + share)
+    edges = [128 * (lanes * edge // edges[-1]) for edge in edges]
+    return [(a, b - a) for a, b in zip(edges[:-1], edges[1:])]
+
+
+def fused(groups, rest_cols, cuts, tails, ids_hbm, levels_hbm, tok_hbm, gate_hbm, up_hbm, down_hbm, out_ref,
           ids_ref, levels_ref, tok, gate_v, up_v, down_v, hid, keep, dsend, drecv, ysend, yrecv, zsend, zrecv,
           send_sem, recv_sem, local_sem):
     rows, width = tok_hbm.shape
@@ -120,14 +128,17 @@
     count = [0]
     endings = []
 
-    def copy_of(i, src, dst, peer):
+    def slots(amount):
+        count[0] += amount
+        return count[0] - amount
+
+    def copy_of(i, j, src, dst, peer):
         return pltpu.make_async_remote_copy(src_ref=src, dst_ref=dst, send_sem=send_sem.at[i],
-                                            recv_sem=recv_sem.at[i], device_id=peer, device_id_type=MESH)
+                                            recv_sem=recv_sem.at[j], device_id=peer, device_id_type=MESH)
 
     def send(src, dst, peer):
-        i = count[0]
-        count[0] += 1
-        copy = copy_of(i, src, dst, peer)
+        i = slots(1)
+        copy = copy_of(i, i, src, dst, peer)
         copy.start()
         endings.append(copy.wait_send)
         return copy
@@ -135,73 +146,78 @@
     def block(group, half, cols):
         return tok.at[group * 2 + half, s, :, pl.ds(cols[0], cols[1])]
 
-    def when_send(group, half, cols, peer, cond):
-        i = count[0]
-        count[0] += 1
+    def do(cond, action):
+        if cond is None:
+            action()
+        else:
+            pl.when(cond)(action)
+
+    def when_send(i, j, group, half, cols, peer, cond=None):
         part_of = block(group, half, cols)
-        copy = copy_of(i, part_of, part_of, peer)
-
-        def do(action):
-            if cond is None:
-                action()
-            else:
-                pl.when(cond)(action)
-        do(copy.start)
-        endings.append(lambda: do(copy.wait_send))
-        return i
-
-    def when_arrived(i, group, half, cols, cond):
+        copy = copy_of(i, j, part_of, part_of, peer)
+        do(cond, copy.start)
+        endings.append(lambda: do(cond, copy.wait_send))
+
+    def when_arrived(j, group, half, cols, cond=None):
         part_of = block(group, half, cols)
-        copy = copy_of(i, part_of, part_of, sub_peer)
-        if cond is None:
-            copy.wait_recv()
-        else:
-            pl.when(cond)(copy.wait_recv)
-
-    def climb(d, half, cols):
-        return (when_send(z - d + 1, half, cols, at(z + 1, h, s), above & (z - d + 1 >= 0)),
-                when_send(z + d - 1, half, cols, at(z - 1, h, s), below & (z + d - 1 < n)))
+        do(cond, copy_of(j, j, part_of, part_of, sub_peer).wait_recv)
+
+    def climb(d, base, half, cols):
+        low, high = z - d + 1, z + d - 1
+        when_send(base + low, base + low, low, half, cols, at(z + 1, h, s), above & (low >= 0))
+        when_send(base + (n if d == 1 else high), base + high, high, half, cols, at(z - 1, h, s), below & (high < n))
 
     crossing, turning = [], []
-
-    def across(group, half, cols, cond=None):
-        crossing.append((when_send(group, half, cols, sub_peer, cond), group, half, cols, cond))
-
-    def turn(group, cols, cond=None):
-        turning.append((when_send(group, h, cols, half_peer, cond), group, 1 - h, cols, cond))
+    front = (0, rest_cols[0][0])
+    back = (front[1], width - front[1])
+    near_base, far_base, back_base = slots(n), slots(n), slots(n)
+    turn_base = [slots(n) for _ in rest_cols]
+
+    def across(base, group, half, cols, cond=None):
+        when_send(base + group, base + group, group, half, cols, sub_peer, cond)
+        crossing.append((base + group, group, half, cols, cond))
+
+    def turn(k, group, cols, cond=None):
+        when_send(turn_base[k] + group, turn_base[k] + group, group, h, cols, half_peer, cond)
+        turning.append((turn_base[k] + group, group, 1 - h, cols, cond))
 
     def turned(amount):
         for _ in range(amount):
             item = turning.pop(0)
             when_arrived(*item)
-            across(*item[1:])
-
-    first_turn = [when_send(z, h, cols, half_peer, None) for cols in first_cols]
-    lines = [(h, cols) for cols in first_cols + rest_cols]
-    steps = [climb(1, half, cols) for half, cols in lines]
-    for cols in rest_cols:
-        turn(z, cols)
-    across(z, h, (0, width))
-    for i, cols in zip(first_turn, first_cols):
-        when_arrived(i, z, 1 - h, cols, None)
-        lines.append((1 - h, cols))
-        steps.append(climb(1, 1 - h, cols))
-        across(z, 1 - h, cols)
+            if item[3] == rest_cols[-1]:
+                across(back_base, item[1], 1 - h, back, item[4])
+
+    first_base = slots(1)
+    when_send(first_base, first_base, z, h, front, half_peer)
+    lines = [(slots(n + 1), h, cols) for cols in rest_cols + [front]]
+    for line in lines:
+        climb(1, *line)
+    for k, cols in enumerate(rest_cols):
+        turn(k, z, cols)
+    across(near_base, z, h, (0, width))
+    when_arrived(first_base, z, 1 - h, front)
+    lines.append((slots(n + 1), 1 - h, front))
+    climb(1, *lines[-1])
+    across(far_base, z, 1 - h, front)
     for d in range(1, n):
-        later = []
         waiting = len(turning)
-        for (half, cols), (rising, falling) in zip(lines, steps):
-            low, high = z - d >= 0, z + d < n
-            when_arrived(rising, z - d, half, cols, low)
-            when_arrived(falling, z + d, half, cols, high)
+        low, high = z - d >= 0, z + d < n
+        for base, half, cols in lines:
+            when_arrived(base + z - d, z - d, half, cols, low)
+            when_arrived(base + z + d, z + d, half, cols, high)
             if d + 1 < n:
-                later.append(climb(d + 1, half, cols))
+                climb(d + 1, base, half, cols)
             if cols in rest_cols:
-                turn(z - d, cols, low)
-                turn(z + d, cols, high)
-            across(z - d, half, cols, low)
-            across(z + d, half, cols, high)
-        steps = later
+                k = rest_cols.index(cols)
+                turn(k, z - d, cols, low)
+                turn(k, z + d, cols, high)
+            elif half is h:
+                across(near_base, z - d, h, (0, width), low)
+                across(near_base, z + d, h, (0, width), high)
+            else:
+                across(far_base, z - d, half, cols, low)
+                across(far_base, z + d, half, cols, high)
         turned(waiting)
     turned(len(turning))
     for item in crossing:
@@ -221,22 +237,38 @@
     ordered = jnp.concatenate([hid[:, half, core].reshape(n * rows, units)
                                for core in (1 - s, s) for half in (1 - h, h)], axis=0).astype(jnp.bfloat16)
 
-    part, span = n * rows, max(size for _, size in cuts)
+    part = n * rows
     d_copies, y_copies, z_copies = [], [], []
-    for c, (start, size) in enumerate(cuts):
+
+    def project(c):
+        start, size = tails[c]
+        cols = pl.ds(start, size)
         terms = jnp.dot(ordered, down_v[:, start:start + size], preferred_element_type=jnp.float32)
-        dsend[c] = terms[:2 * part].astype(jnp.bfloat16)
-        keep[c] = terms[2 * part:]
-        d_copies.append(send(dsend.at[c], drecv.at[c], sub_peer))
-    for c in range(len(cuts)):
+        dsend[:, cols] = terms[:2 * part].astype(jnp.bfloat16)
+        keep[:, cols] = terms[2 * part:]
+        d_copies.append(send(dsend.at[:, cols], drecv.at[:, cols], sub_peer))
+
+    def join_cores(c):
+        cols = pl.ds(*tails[c])
         d_copies[c].wait_recv()
-        ysend[c] = (keep[c, :part] + drecv[c, :part].astype(jnp.float32)).astype(jnp.bfloat16)
-        y_copies.append(send(ysend.at[c], yrecv.at[c], half_peer))
-    for c in range(len(cuts)):
+        ysend[:, cols] = (keep[:part, cols] + drecv[:part, cols].astype(jnp.float32)).astype(jnp.bfloat16)
+        y_copies.append(send(ysend.at[:, cols], yrecv.at[:, cols], half_peer))
+
+    def join_halves(c):
+        cols = pl.ds(*tails[c])
         y_copies[c].wait_recv()
-        sums = (keep[c, part:] + drecv[c, part:].astype(jnp.float32)) + yrecv[c].astype(jnp.float32)
-        zsend[c] = sums.reshape(n, rows, span).astype(jnp.bfloat16)
-        z_copies.append([send(zsend.at[c, ring(d)], zrecv.at[c, d], at(ring(d), h, s)) for d in range(1, n)])
+        sums = keep[part:, cols] + drecv[part:, cols].astype(jnp.float32) + yrecv[:, cols].astype(jnp.float32)
+        zsend[:, :, cols] = sums.reshape(n, rows, tails[c][1]).astype(jnp.bfloat16)
+        z_copies.append([send(zsend.at[ring(d), :, cols], zrecv.at[d, :, cols], at(ring(d), h, s))
+                         for d in range(1, n)])
+
+    for c in range(len(tails) + 2):
+        if c < len(tails):
+            project(c)
+        if c >= 2:
+            join_cores(c - 2)
+    for c in range(len(tails)):
+        join_halves(c)
     levels = levels_ref[...].astype(jnp.float32)
     shares = levels / jnp.sum(levels, axis=0, keepdims=True)
     ids = ids_ref[...]
@@ -245,12 +277,13 @@
     for d in range(n):
         flat = jnp.sum(jnp.where(ids == ring(-d), shares, 0.0), axis=0, keepdims=True)
         weights.append(jnp.sum(jnp.where(eye, flat, 0.0), axis=1, keepdims=True))
-    for c, (start, size) in enumerate(cuts):
-        mixed = weights[0] * zsend[c, z].astype(jnp.float32)
+    for c, (start, size) in enumerate(tails):
+        cols = pl.ds(start, size)
+        mixed = weights[0] * zsend[z, :, cols].astype(jnp.float32)
         for d in range(1, n):
             z_copies[c][d - 1].wait_recv()
-            mixed += weights[d] * zrecv[c, d].astype(jnp.float32)
-        out_ref[:, start:start + size] = mixed.astype(out_ref.dtype)
+            mixed += weights[d] * zrecv[d, :, cols].astype(jnp.float32)
+        out_ref[:, cols] = mixed.astype(out_ref.dtype)
     for ending in endings:
         ending()
 
@@ -261,13 +294,16 @@
     units = gate_proj.shape[2]
     pieces = 7
     cuts = column_cuts(width, pieces)
-    nc, span, part = len(cuts), cuts[0][1], n * rows
+    span, part = cuts[0][1], n * rows
+    tails = shrinking_cuts(width)
+    nc = len(tails)
     bf, f32 = jnp.bfloat16, jnp.float32
     vmem = pl.BlockSpec(memory_space=pltpu.VMEM)
     hbm = pl.BlockSpec(memory_space=pl.ANY)
-    messages = 240
+    rest = column_cuts_from(span, width, 3)
+    messages = (3 + len(rest)) * n + (len(rest) + 2) * (n + 1) + 1 + nc * (n + 1)
     return pl.pallas_call(
-        functools.partial(fused, n, [cuts[0]], column_cuts_from(cuts[0][1], width, 3), cuts),
+        functools.partial(fused, n, rest, cuts, tails),
         out_shape=jax.ShapeDtypeStruct((rows, width), bf),
         in_specs=[hbm] * 6,
         out_specs=vmem,
@@ -279,13 +315,13 @@
             pltpu.VMEM((width, units), bf),
             pltpu.VMEM((units, width), bf),
             pltpu.VMEM((n, 2, 2, rows, units), f32),
-            pltpu.VMEM((nc, 2 * part, span), f32),
-            pltpu.VMEM((nc, 2 * part, span), bf),
-            pltpu.VMEM((nc, 2 * part, span), bf),
-            pltpu.VMEM((nc, part, span), bf),
-            pltpu.VMEM((nc, part, span), bf),
-            pltpu.VMEM((nc, n, rows, span), bf),
-            pltpu.VMEM((nc, n, rows, span), bf),
+            pltpu.VMEM((2 * part, width), f32),
+            pltpu.VMEM((2 * part, width), bf),
+            pltpu.VMEM((2 * part, width), bf),
+            pltpu.VMEM((part, width), bf),
+            pltpu.VMEM((part, width), bf),
+            pltpu.VMEM((n, rows, width), bf),
+            pltpu.VMEM((n, rows, width), bf),
             pltpu.SemaphoreType.DMA((messages,)),
             pltpu.SemaphoreType.DMA((messages,)),
             pltpu.SemaphoreType.DMA((6,)),

time: 43.4 us -> 39.8 us (0.917)
  Pallas kernels: 41.7 us -> 38.1 us
    pallas_call x1, Pallas kernels: 41.7 us -> 38.1 us  [fused_local(): pl.pallas_call(functools.partial(fused, n, rest, cuts, tails), out_shape=...]
where the time goes in v3:
time: 39.8 us; the launch traced here: 39.6 us
  Pallas kernels  38.1 us (96%)
  local copies, waits for them, and re-layouts  1.55 us (4%)
    pallas_call x1, Pallas kernels, fused_local(): pl.pallas_call(functools.partial(fused, n, rest, cuts, tails), out_shape=...  38.1 us
    unnamed x1, local copies, waits for them, and re-layouts  1.55 us

profile of v3, /device:TPU:0, one launch (start us, length us, event | category | flops | bytes accessed | tf_op | source)
XLA Modules:
  0.0 39.6 jit_solution(10507535386840863542)
XLA Ops:
  0.0 38.1 %shard_map.64 = bf16[8,7168]{1,0:T(8,128)(2,1)} custom-call(s32[2,8]{1,0:T(2,128)} %bitcast.2, s32[2,8]{1,0:T(2,128)} %bitcast.3, bf16[8,7168]{1,0:T(8,128)(2,1)} %tok_hbm.1, bf16[1,7168,256]{2,1,0:T(8,128)(2,1)} %gate_hbm.1, bf16[1,7168,256]{2,1,0:T(8,128)(2,1)} %up_hbm.1, bf16[1,256,7168]{2,1,0:T(8,128)(2,1)} %down_hbm.1), custom_call_target="tpu_custom_call" | custom-call | tf_op jit(solution)/shard_map/pallas_call | solution.py:305
  38.1 1.6 %copy.8 = bf16[8,7168]{1,0:T(8,128)(2,1)} copy(bf16[8,7168]{1,0:T(8,128)(2,1)} %shard_map.64) | data formatting | bytes 229376
